TPU v7x, 32 devices: a whole 2x2x4 slice. The times are simulated.
32 devices in a mesh: chan: 4 (over y, x), rows: 8 (over z, core).
Axes of the slice: x: 2, y: 2, z: 4, core: 2. Of those that a mesh axis runs over, the one named last changes fastest.
Arguments:
- residual: float32 [4, 256, 16384], P('chan', 'rows'), may hold values from -6 to 6
- psf: float32 [4, 2048, 2048], P('chan', 'rows'), may hold values from -2 to 2
- positions: int32 [32, 2], replicated, may hold values from 0 to 15360, as said below
Outputs:
- residual_out: float32 [4, 256, 16384], P('chan', 'rows')
- normalized: float32 [256, 16384], P('rows', 'chan')
Inputs may be any that keep to these rules, and one draw needn't show every extreme that they name: positions[k, 0] is a row of the image, 0 to 255; positions[k, 1] is a column from 1024 to 15360.
All inputs are finite; a program needn't handle non-finite values.
Results may differ from a plain program's by a relative error of at most 0.0001.
Values sent between devices are 32-bit elements; how exact they have to be, the bound alone decides.
A program may use at most 128 MiB of HBM per device.

v0:
```python
import jax
import jax.numpy as jnp
from jax import lax
from jax.sharding import PartitionSpec as P

STEPS = 32


def on_device(residual, psf, positions):
    chan_id = lax.axis_index("chan")
    nchan = lax.axis_size("chan")
    row_id = lax.axis_index("rows")
    nrows = lax.axis_size("rows")
    slab = residual.shape[1]
    ncols = residual.shape[2]
    own_psf = psf[0]
    shard_rows = own_psf.shape[0]
    patch = own_psf.shape[1]
    half = patch // 2
    first = row_id * slab
    chan_hot = (jnp.arange(nchan) == chan_id).astype(jnp.float32)
    full_psf = lax.all_gather(own_psf, "rows", axis=0, tiled=True)
    padded_psf = jnp.pad(full_psf, ((slab, slab), (0, 0)))
    zero = jnp.int32(0)

    def subtract(image, row, col, amount):
        offset = first - row + half
        touches = jnp.logical_and(offset > -slab, offset < patch)
        start = jnp.clip(offset + slab, 0, patch + slab)
        psf_rows = lax.dynamic_slice(padded_psf, (start, zero), (slab, patch))
        window = lax.dynamic_slice(image, (zero, col - half), (slab, patch))
        scale = jnp.where(touches, amount, 0.0)
        return lax.dynamic_update_slice(image, window - scale * psf_rows, (zero, col - half))

    image = residual[0]
    peak_rows = positions[:, 0]
    peak_cols = positions[:, 1]
    inside = jnp.logical_and(peak_rows >= first, peak_rows < first + slab)
    local_rows = jnp.clip(peak_rows - first, 0, slab - 1)
    start_values = jnp.where(inside, image[local_rows, peak_cols], 0.0)
    row_offset = peak_rows[:, None] - peak_rows[None, :] + half - row_id * shard_rows
    col_offset = peak_cols[:, None] - peak_cols[None, :] + half
    owned = (row_offset >= 0) & (row_offset < shard_rows) & (col_offset >= 0) & (col_offset < patch)
    couple = own_psf[jnp.clip(row_offset, 0, shard_rows - 1), jnp.clip(col_offset, 0, patch - 1)]
    couple = jnp.where(owned, couple, 0.0)
    start_table, couple_table = lax.psum(
        (chan_hot[:, None] * start_values[None, :], chan_hot[:, None, None] * couple[None, :, :]),
        ("chan", "rows"),
    )

    def solve(k, amps):
        taken = jnp.sum(amps * lax.dynamic_index_in_dim(couple_table, k, 1, False), axis=1)
        value = lax.dynamic_index_in_dim(start_table, k, 1, False) - taken
        amp = 0.25 * (value + jnp.sum(value) / nchan)
        return lax.dynamic_update_index_in_dim(amps, amp, k, 1)

    amps = lax.fori_loop(0, STEPS, solve, jnp.zeros((nchan, STEPS), jnp.float32))
    own_amps = jnp.sum(chan_hot[:, None] * amps, axis=0)

    def apply(k, image):
        return subtract(image, positions[k, 0], positions[k, 1], own_amps[k])

    image = lax.fori_loop(0, STEPS, apply, image)
    count = slab * nrows * ncols
    parts = lax.psum_scatter(image, "chan", scatter_dimension=1, tiled=True)
    total = lax.psum(jnp.sum(parts * parts), ("chan", "rows"))
    normalized = parts * lax.rsqrt(total / count + 1e-06)
    return (image[None], normalized)


def solution(mesh):
    return jax.shard_map(
        on_device,
        mesh=mesh,
        in_specs=(P("chan", "rows", None), P("chan", "rows", None), P()),
        out_specs=(P("chan", "rows", None), P("rows", "chan")),
        check_vma=False,
    )
```

profile of v0, /device:TPU:0, one launch (start us, length us, event | category | flops | bytes accessed | tf_op | source)
XLA Modules:
  0.0 488.9 jit_solution(8474311670628880495)
XLA Ops:
  7.2 3.0 copy.28
  11.9 8.6 %gather_fusion.1 = f32[1024]{0:T(1024)S(1)} fusion(f32[256,2048]{1,0:T(8,128)S(1)} %bitcast.46, s32[1024]{0:T(1024)S(1)} %reshape.252), kind=kCustom, calls=%fused_computation.1 | custom fusion | bytes 16384 | tf_op jit(solution)/shard_map/gather | solution.py:44
  22.5 50.0 %all-reduce.1 = (f32[4,32]{1,0:T(4,128)S(1)}, f32[4,32,32]{2,0,1:T(4,128)S(1)}) all-reduce(f32[4,32]{1,0:T(4,128)S(1)} %broadcast_multiply_fusion.2, f32[4,32,32]{2,0,1:T(4,128)S(1)} %broadcast_multiply_fusion.1), channel_id=1, replica_groups=mesh['chan'=4,'rows'=8] {'chan','rows'}, use_global_device_ids=true, to_apply=%region_1.2 | all-reduce | flops 4224 | bytes 33792 | tf_op jit(solution)/shard_map/psum | solution.py:46
  72.5 57.8 %while.30 = (s32[]{:T(128)}, f32[4,32]{1,0:T(4,128)S(1)}, f32[4,32]{1,0:T(4,128)S(1)}, f32[4,32,32]{2,0,1:T(4,128)S(1)}, s32[]{:T(128)}, /*index=5*/f32[]{:T(128)}, s32[]{:T(128)}) while((s32[]{:T(128)}, f32[4,32]{1,0:T(4,128)S(1)}, f32[4,32]{1,0:T(4,128)S(1)}, f32[4,32,32]{2,0,1:T(4,128)S(1)}, s32[]{:T(128)}, /*index=5*/f32[]{:T(128)}, ...), condition=%wide.region_5.6_spmd, body=%wide.region_2.5_spmd.sunk | while | flops 274 | bytes 2329 | solution.py:57
  130.4 34.9 %all-gather.3.cloned.1.call-done = f32[1,2048,2048]{2,1,0:T(8,128)} async-done(((f32[1,256,2048]{2,1,0:T(8,128)}), f32[1,2048,2048]{2,1,0:T(8,128)}) %all-gather.3.cloned.1.call-update) | async-done | bytes 16777232 | tf_op jit(solution)/shard_map/all_gather | solution.py:22
  165.3 11.7 %pad.4 = f32[2112,2048]{1,0:T(8,128)} pad(f32[2048,2048]{1,0:T(8,128)} %bitcast.50, f32[]{:T(128)} %constant.206.clone.1), padding=32_32x0_0 | pad | bytes 34078724 | tf_op jit(solution)/shard_map/jit(_pad)/pad | solution.py:23
  177.0 227.6 %while.31 = (s32[]{:T(128)}, f32[32,16384]{1,0:T(8,128)}, s32[32,2]{0,1:T(2,128)S(1)}, s32[]{:T(128)}, f32[32]{0:T(128)S(1)}, /*index=5*/f32[2112,2048]{1,0:T(8,...) while((s32[]{:T(128)}, f32[32,16384]{1,0:T(8,128)}, ...), condition=%wide.region_8.9_spmd, body=%wide.region_7.8_spmd.sunk | while | flops 131087 | bytes 1311065 | solution.py:63
  182.1 2.0 dynamic_update_slice.24
  189.2 2.0 dynamic_update_slice.24
  196.4 2.0 dynamic_update_slice.24
  203.5 2.0 dynamic_update_slice.24
  210.6 2.0 dynamic_update_slice.24
  217.8 2.0 dynamic_update_slice.24
  224.9 2.0 dynamic_update_slice.24
  232.0 2.0 dynamic_update_slice.24
  239.2 2.0 dynamic_update_slice.24
  246.3 2.0 dynamic_update_slice.24
  253.4 2.0 dynamic_update_slice.24
  260.5 2.0 dynamic_update_slice.24
  267.7 2.0 dynamic_update_slice.24
  274.8 2.0 dynamic_update_slice.24
  281.9 2.0 dynamic_update_slice.24
  296.2 2.0 dynamic_update_slice.24
  303.3 2.0 dynamic_update_slice.24
  317.5 2.0 dynamic_update_slice.24
  324.6 2.0 dynamic_update_slice.24
  331.7 2.0 dynamic_update_slice.24
  338.9 2.0 dynamic_update_slice.24
  352.8 2.0 dynamic_update_slice.24
  359.9 2.0 dynamic_update_slice.24
  404.7 33.5 %reduce-scatter.2.cloned.1.call-done = f32[32,4096]{1,0:T(8,128)} async-done(((f32[32,16384]{1,0:T(8,128)}), f32[32,4096]{1,0:T(8,128)}) %reduce-scatter.2.cloned.1.call-update) | async-done | bytes 524304 | tf_op jit(solution)/shard_map/reduce_scatter | solution.py:65
  440.0 39.5 %psum.23 = f32[]{:T(128)} all-reduce(f32[]{:T(128)} %multiply_reduce_fusion), channel_id=1, replica_groups=mesh['chan'=4,'rows'=8] {'chan','rows'}, use_global_device_ids=true, to_apply=%region_11.12 | all-reduce | flops 1 | bytes 8 | tf_op jit(solution)/shard_map/psum | solution.py:66
  (319 shorter events, 138.5 us)
Async XLA Ops:
  7.2 158.1 %all-gather.3.cloned.1.call-start = ((), (), s32[]{:S(2)}) async-start(), calls=%async_computation.2 | async-start | bytes 18874368 | tf_op jit(solution)/shard_map/all_gather | solution.py:22
  10.3 0.7 copy-start.1
  10.3 1.6 copy-start
  10.3 427.9 %reduce-scatter.2.cloned.1.call-start = ((), (), s32[]{:S(2)}) async-start(), calls=%async_computation.1 | async-start | bytes 2621440 | tf_op jit(solution)/shard_map/reduce_scatter | solution.py:65
Sparse Core Ops, SparseCore 0:
  10.4 154.8 all-gather.2
  404.8 33.3 reduce-scatter.1
where the time goes:
time: 492 us; the launch traced here: 489 us
  local copies, waits for them, and re-layouts  140 us (28%)
  loops' own time  108 us (22%)
  blocking collectives  89.5 us (18%)
  other arithmetic  68.9 us (14%)
  waiting for transfers between devices  68.4 us (14%)
  between operations  14.8 us (3%)
    another operation x1, loops' own time, on_device(): image = lax.fori_loop(0, STEPS, apply, image)  85.1 us
    dynamic_update_slice x32, local copies, waits for them, and re-layouts, subtract(): lax.dynamic_update_slice(image, window - scale * psf_rows, (zero, col - h...  64.5 us
    psum x1, blocking collectives, on_device(): lax.psum((chan_hot[:, None] * start_values[None, :], chan_hot[:, None, No...  50 us
    dynamic_slice x64, local copies, waits for them, and re-layouts, apply(): return subtract(image, positions[k, 0], positions[k, 1], own_amps[k])  39.7 us
    psum x1, blocking collectives, on_device(): total = lax.psum(jnp.sum(parts * parts), ('chan', 'rows'))  39.5 us
    sub x32, other arithmetic, subtract(): window - scale * psf_rows  38.4 us
    all_gather x1, waiting for transfers between devices, on_device(): full_psf = lax.all_gather(own_psf, 'rows', axis=0, tiled=True)  34.9 us
    reduce_scatter x1, waiting for transfers between devices, on_device(): parts = lax.psum_scatter(image, 'chan', scatter_dimension=1, tiled=True)  33.5 us
  transfers between devices with their start and end apart: 2, of which 2 were waited for; matrix products, arithmetic and copies ran while one was open for 9% of the time, Pallas kernels for 0%

commit v1 on v0

--- a/solution.py
+++ b/solution.py
@@ -7,6 +7,33 @@
 
 
 def on_device(residual, psf, positions):
+
+    def finish_members_all(vec):
+        low = lax.axis_size("rows")
+        o_now = lax.axis_index("rows")
+        field_out, side_arr, response = (low, o_now, vec.shape[0])
+        g_now = jnp.zeros(
+            tuple((h * field_out if c == 0 else h for c, h in enumerate(vec.shape))), vec.dtype
+        )
+        y_new = next_value = vec
+        at = 1
+        k_now = lax.dynamic_update_slice_in_dim(g_now, vec, side_arr * response, axis=0)
+        while at < field_out // 2 + 1:
+            y_new = lax.ppermute(
+                y_new, "rows", tuple(((c, (c + 1) % field_out) for c in range(field_out)))
+            )
+            k_now = lax.dynamic_update_slice_in_dim(
+                k_now, y_new, (side_arr - at) % field_out * response, axis=0
+            )
+            if 2 * at < field_out:
+                clean = tuple(((c, (c - 1) % field_out) for c in range(field_out)))
+                next_value = lax.ppermute(next_value, "rows", clean)
+                k_now = lax.dynamic_update_slice_in_dim(
+                    k_now, next_value, (side_arr + at) % field_out * response, axis=0
+                )
+            at += 1
+        return k_now
+
     chan_id = lax.axis_index("chan")
     nchan = lax.axis_size("chan")
     row_id = lax.axis_index("rows")
@@ -19,7 +46,7 @@
     half = patch // 2
     first = row_id * slab
     chan_hot = (jnp.arange(nchan) == chan_id).astype(jnp.float32)
-    full_psf = lax.all_gather(own_psf, "rows", axis=0, tiled=True)
+    full_psf = finish_members_all(own_psf)
     padded_psf = jnp.pad(full_psf, ((slab, slab), (0, 0)))
     zero = jnp.int32(0)
 

time: 492 us -> 548 us (1.11)
  local copies, waits for them, and re-layouts: 140 us -> 168 us
  waiting for transfers between devices: 68.4 us -> 92.1 us
  starting transfers between devices: 0.08 us -> 12 us
  blocking collectives: 89.5 us -> 79.3 us
    ppermute x0 -> x7, waiting for transfers between devices: none -> 58.7 us  [the longest x4 58.2 us: finish_members_all(): lax.ppermute(y_new, 'rows', tuple(((c, (c + 1) % field_out) for c in rang...]
    all_gather x1 -> x0, waiting for transfers between devices: 34.9 us -> none  [on_device(): full_psf = lax.all_gather(own_psf, 'rows', axis=0, tiled=True)]
    gather x2, local copies, waits for them, and re-layouts: 8.65 us -> 26.9 us  [on_device(): own_psf[jnp.clip(row_offset, 0, shard_rows - 1), jnp.clip(col_offset, 0,...]
    ppermute x0 -> x7, starting transfers between devices: none -> 11.9 us  [the longest x3 11.3 us: finish_members_all(): next_value = lax.ppermute(next_value, 'rows', clean)]
    dynamic_update_slice x0 -> x8, local copies, waits for them, and re-layouts: none -> 11.2 us  [the longest x4 5.62 us: finish_members_all(): lax.dynamic_update_slice_in_dim(k_now, y_new, (side_arr - at) % field_out...]
    psum x1, blocking collectives: 50 us -> 39.9 us  [on_device(): lax.psum((chan_hot[:, None] * start_values[None, :], chan_hot[:, None, No...]
  transfers between devices with their start and end apart: 2 -> 8, of which waited for: 2 -> 4; matrix products, arithmetic and copies ran while one was open for 9% -> 14% of each run, Pallas kernels for 0% -> 0%
where the time goes in v1:
time: 548 us; the launch traced here: 543 us
  local copies, waits for them, and re-layouts  168 us (31%)
  loops' own time  109 us (20%)
  waiting for transfers between devices  92.1 us (17%)
  blocking collectives  79.3 us (14%)
  other arithmetic  68 us (12%)
  between operations  15 us (3%)
  starting transfers between devices  12 us (2%)
    another operation x1, loops' own time, on_device(): image = lax.fori_loop(0, STEPS, apply, image)  89.5 us
    dynamic_update_slice x32, local copies, waits for them, and re-layouts, subtract(): lax.dynamic_update_slice(image, window - scale * psf_rows, (zero, col - h...  64.5 us
    ppermute x4, waiting for transfers between devices, finish_members_all(): lax.ppermute(y_new, 'rows', tuple(((c, (c + 1) % field_out) for c in rang...  58.2 us
    dynamic_slice x64, local copies, waits for them, and re-layouts, apply(): return subtract(image, positions[k, 0], positions[k, 1], own_amps[k])  42.9 us
    psum x1, blocking collectives, on_device(): lax.psum((chan_hot[:, None] * start_values[None, :], chan_hot[:, None, No...  39.9 us
    psum x1, blocking collectives, on_device(): total = lax.psum(jnp.sum(parts * parts), ('chan', 'rows'))  39.5 us
    sub x32, other arithmetic, subtract(): window - scale * psf_rows  38.4 us
    reduce_scatter x1, waiting for transfers between devices, on_device(): parts = lax.psum_scatter(image, 'chan', scatter_dimension=1, tiled=True)  33.4 us
  transfers between devices with their start and end apart: 8, of which 4 were waited for; matrix products, arithmetic and copies ran while one was open for 14% of the time, Pallas kernels for 0%

profile of v1, /device:TPU:0, one launch (start us, length us, event | category | flops | bytes accessed | tf_op | source)
XLA Modules:
  0.0 543.3 jit_solution(2489638532302241455)
XLA Ops:
  7.2 3.0 copy.36
  10.8 4.0 collective-permute-start.1
  14.8 43.9 %collective-permute-done = f32[256,2048]{1,0:T(8,128)} collective-permute-done((f32[256,2048]{1,0:T(8,128)}, f32[256,2048]{1,0:T(8,128)}, u32[]{:S(2)}, u32[]{:S(2)}) %collective-permute-start) | collective-permute-done | bytes 2097184 | tf_op jit(solution)/shard_map/ppermute | solution.py:22
  59.1 3.8 collective-permute-start.3
  63.8 26.9 %gather_fusion.1 = f32[1024]{0:T(1024)S(1)} fusion(f32[256,2048]{1,0:T(8,128)} %bitcast.48, s32[1024]{0:T(1024)S(1)} %reshape.252), kind=kCustom, calls=%fused_computation.1 | custom fusion | bytes 16384 | tf_op jit(solution)/shard_map/gather | solution.py:71
  92.7 39.9 %all-reduce.1 = (f32[4,32]{1,0:T(4,128)S(1)}, f32[4,32,32]{2,0,1:T(4,128)S(1)}) all-reduce(f32[4,32]{1,0:T(4,128)S(1)} %broadcast_multiply_fusion.2, f32[4,32,32]{2,0,1:T(4,128)S(1)} %broadcast_multiply_fusion.1), channel_id=1, replica_groups=mesh['chan'=4,'rows'=8] {'chan','rows'}, use_global_device_ids=true, to_apply=%region_1.2 | all-reduce | flops 4224 | bytes 33792 | tf_op jit(solution)/shard_map/psum | solution.py:73
  132.6 3.5 collective-permute-start.5
  136.1 53.4 %while.30 = (s32[]{:T(128)}, f32[4,32]{1,0:T(4,128)S(1)}, f32[4,32]{1,0:T(4,128)S(1)}, f32[4,32,32]{2,0,1:T(4,128)S(1)}, s32[]{:T(128)}, /*index=5*/f32[]{:T(128)}, s32[]{:T(128)}) while((s32[]{:T(128)}, f32[4,32]{1,0:T(4,128)S(1)}, f32[4,32]{1,0:T(4,128)S(1)}, f32[4,32,32]{2,0,1:T(4,128)S(1)}, s32[]{:T(128)}, /*index=5*/f32[]{:T(128)}, ...), condition=%wide.region_5.6_spmd, body=%wide.region_2.5_spmd.sunk | while | flops 274 | bytes 2321 | solution.py:84
  189.8 2.1 broadcast_in_dim.33
  202.9 14.3 %collective-permute-done.6 = f32[256,2048]{1,0:T(8,128)S(1)} collective-permute-done((f32[256,2048]{1,0:T(8,128)}, f32[256,2048]{1,0:T(8,128)S(1)}, u32[]{:S(2)}, u32[]{:S(2)}) %collective-permute-start.6) | collective-permute-done | bytes 2097184 | tf_op jit(solution)/shard_map/ppermute | solution.py:22
  217.5 6.4 %pad.4 = f32[2112,2048]{1,0:T(8,128)} pad(f32[2048,2048]{1,0:T(8,128)S(1)} %constant_dynamic-update-slice_fusion, f32[]{:T(128)} %constant.250.clone.1), padding=32_32x0_0 | pad | bytes 34078724 | tf_op jit(solution)/shard_map/jit(_pad)/pad | solution.py:50
  223.9 235.3 %while.31 = (s32[]{:T(128)}, f32[32,16384]{1,0:T(8,128)}, s32[32,2]{0,1:T(2,128)S(1)}, s32[]{:T(128)}, f32[32]{0:T(128)S(1)}, /*index=5*/f32[2112,2048]{1,0:T(8,...) while((s32[]{:T(128)}, f32[32,16384]{1,0:T(8,128)}, ...), condition=%wide.region_8.9_spmd, body=%wide.region_7.8_spmd.sunk | while | flops 131087 | bytes 1311057 | solution.py:90
  229.3 2.0 dynamic_update_slice.64
  236.6 2.0 dynamic_update_slice.64
  244.0 2.0 dynamic_update_slice.64
  251.4 2.0 dynamic_update_slice.64
  258.7 2.0 dynamic_update_slice.64
  266.1 2.0 dynamic_update_slice.64
  273.5 2.0 dynamic_update_slice.64
  280.9 2.0 dynamic_update_slice.64
  288.2 2.0 dynamic_update_slice.64
  295.6 2.0 dynamic_update_slice.64
  303.0 2.0 dynamic_update_slice.64
  310.3 2.0 dynamic_update_slice.64
  317.7 2.0 dynamic_update_slice.64
  325.1 2.0 dynamic_update_slice.64
  332.4 2.0 dynamic_update_slice.64
  347.2 2.0 dynamic_update_slice.64
  354.5 2.0 dynamic_update_slice.64
  369.2 2.0 dynamic_update_slice.64
  459.3 33.4 %reduce-scatter.2.cloned.1.call-done = f32[32,4096]{1,0:T(8,128)} async-done(((f32[32,16384]{1,0:T(8,128)}), f32[32,4096]{1,0:T(8,128)}) %reduce-scatter.2.cloned.1.call-update) | async-done | bytes 524304 | tf_op jit(solution)/shard_map/reduce_scatter | solution.py:92
  494.4 39.5 %psum.23 = f32[]{:T(128)} all-reduce(f32[]{:T(128)} %multiply_reduce_fusion), channel_id=1, replica_groups=mesh['chan'=4,'rows'=8] {'chan','rows'}, use_global_device_ids=true, to_apply=%region_11.12 | all-reduce | flops 1 | bytes 8 | tf_op jit(solution)/shard_map/psum | solution.py:93
  (339 shorter events, 161.7 us)
Async XLA Ops:
  7.2 85.2 %copy-start.1 = (s32[32,2]{0,1:T(2,128)S(1)}, s32[32,2]{0,1:T(2,128)}, u32[]{:S(2)}) copy-start(s32[32,2]{0,1:T(2,128)} %param.9) | copy-start | bytes 772
  7.2 485.5 %reduce-scatter.2.cloned.1.call-start = ((), (), s32[]{:S(2)}) async-start(), calls=%async_computation.1 | async-start | bytes 2621440 | tf_op jit(solution)/shard_map/reduce_scatter | solution.py:92
  10.3 48.4 %collective-permute-start = (f32[256,2048]{1,0:T(8,128)}, f32[256,2048]{1,0:T(8,128)}, u32[]{:S(2)}, u32[]{:S(2)}) collective-permute-start(f32[256,2048]{1,0:T(8,128)} %bitcast.46), channel_id=1, source_target_pairs={{0,1},{1,2},{2,3},{3,4},{4,5},{5,6},{6,7},{7,0},{8,9},{9,10},{10,1... | collective-permute-start | bytes 6291464 | tf_op jit(solution)/shard_map/ppermute | solution.py:22
  10.8 48.4 %collective-permute-start.1 = (f32[256,2048]{1,0:T(8,128)}, f32[256,2048]{1,0:T(8,128)}, u32[]{:S(2)}, u32[]{:S(2)}) collective-permute-start(f32[256,2048]{1,0:T(8,128)} %bitcast.47), channel_id=1, source_target_pairs={{0,7},{1,0},{2,1},{3,2},{4,3},{5,4},{6,5},{7,6},{8,15},{9,8},{10,9... | collective-permute-start | bytes 6291464 | tf_op jit(solution)/shard_map/ppermute | solution.py:30
  58.7 73.8 %collective-permute-start.2 = (f32[256,2048]{1,0:T(8,128)}, f32[256,2048]{1,0:T(8,128)}, u32[]{:S(2)}, u32[]{:S(2)}) collective-permute-start(f32[256,2048]{1,0:T(8,128)} %collective-permute-done), channel_id=1, source_target_pairs={{0,1},{1,2},{2,3},{3,4},{4,5},{5,6},{6,7},{7,0},{8,9},{9,10},{10,1... | collective-permute-start | bytes 6291464 | tf_op jit(solution)/shard_map/ppermute | solution.py:22
  59.1 73.5 %collective-permute-start.3 = (f32[256,2048]{1,0:T(8,128)}, f32[256,2048]{1,0:T(8,128)}, u32[]{:S(2)}, u32[]{:S(2)}) collective-permute-start(f32[256,2048]{1,0:T(8,128)} %collective-permute-done.1), channel_id=1, source_target_pairs={{0,7},{1,0},{2,1},{3,2},{4,3},{5,4},{6,5},{7,6},{8,15},{9,8},{10,9... | collective-permute-start | bytes 6291464 | tf_op jit(solution)/shard_map/ppermute | solution.py:30
  63.8 128.1 %copy-start = (f32[1,256,2048]{2,1,0:T(8,128)S(1)}, f32[1,256,2048]{2,1,0:T(8,128)}, u32[]{:S(2)}) copy-start(f32[1,256,2048]{2,1,0:T(8,128)} %param.8) | copy-start | bytes 6291460
  132.5 57.2 %collective-permute-start.4 = (f32[256,2048]{1,0:T(8,128)}, f32[256,2048]{1,0:T(8,128)}, u32[]{:S(2)}, u32[]{:S(2)}) collective-permute-start(f32[256,2048]{1,0:T(8,128)} %collective-permute-done.2), channel_id=1, source_target_pairs={{0,1},{1,2},{2,3},{3,4},{4,5},{5,6},{6,7},{7,0},{8,9},{9,10},{10,1... | collective-permute-start | bytes 6291464 | tf_op jit(solution)/shard_map/ppermute | solution.py:22
  132.6 68.5 %collective-permute-start.5 = (f32[256,2048]{1,0:T(8,128)}, f32[256,2048]{1,0:T(8,128)}, u32[]{:S(2)}, u32[]{:S(2)}) collective-permute-start(f32[256,2048]{1,0:T(8,128)} %collective-permute-done.3), channel_id=1, source_target_pairs={{0,7},{1,0},{2,1},{3,2},{4,3},{5,4},{6,5},{7,6},{8,15},{9,8},{10,9... | collective-permute-start | bytes 6291464 | tf_op jit(solution)/shard_map/ppermute | solution.py:30
  189.7 27.5 %collective-permute-start.6 = (f32[256,2048]{1,0:T(8,128)}, f32[256,2048]{1,0:T(8,128)S(1)}, u32[]{:S(2)}, u32[]{:S(2)}) collective-permute-start(f32[256,2048]{1,0:T(8,128)} %collective-permute-done.4), channel_id=1, source_target_pairs={{0,1},{1,2},{2,3},{3,4},{4,5},{5,6},{6,7},{7,0},{8,9},{9,10},{10,1... | collective-permute-start | bytes 6291464 | tf_op jit(solution)/shard_map/ppermute | solution.py:22
Sparse Core Ops, SparseCore 0:
  459.4 33.2 reduce-scatter.1
